TPU v7x, 32 devices: a whole 2x2x4 slice. The times are simulated.
32 devices in a mesh: tok: 4 (over y, x), row: 2 (over core), col: 4 (over z).
Axes of the slice: x: 2, y: 2, z: 4, core: 2. Of those that a mesh axis runs over, the one named last changes fastest.
Arguments:
- activations: bfloat16 [2048, 4096], P(('tok', 'col'), 'row'), may hold values from -6 to 6
- grads_t: bfloat16 [4, 7392, 2048], P(None, 'col', ('tok', 'row')), may hold values from -0.14941406 to 0.14941406
Outputs:
- weight_grad: float32 [4, 7392, 4096], P('tok', 'col', 'row')
All inputs are finite; a program needn't handle non-finite values.
Results may differ from a plain program's by a relative error of at most 0.0003.
Values may be sent and summed in bfloat16 or wider, within the bound.
A program may use at most 128 MiB of HBM per device.

v0:
```python
import functools

import jax
import jax.numpy as jnp
from jax import lax
from jax.experimental import pallas as pl
from jax.experimental.pallas import tpu as pltpu
from jax.sharding import PartitionSpec as P

MESH = pl.DeviceIdType.MESH


def ring_map(place, n):
    if n % 4:
        return place
    return place + ((place % 4) // 2) * (1 - 2 * (place % 2))


def kernel(n, m, acts, grads, every, held, stage, stage_g,
           local_sem, zsend, zrecv, rsend, rrecv, gsend, grecv, psend):
    k, r, c = lax.axis_index("tok"), lax.axis_index("row"), lax.axis_index("col")
    place = ring_map(k, n)
    rows, wide = acts.shape
    quarter = wide // 4
    chunk = grads.shape[2]
    up, down = c + 1 < m, c > 0
    reach = ((n // 2, n - 1 - n // 2), (n - 1 - n // 2, n // 2))
    hops = n // 2

    def member(offset):
        return ring_map((place + offset + 2 * n) % n, n)

    barrier = pltpu.get_barrier_semaphore()
    for j in range(1, n):
        pl.semaphore_signal(barrier, inc=1, device_id={"tok": (k + j) % n}, device_id_type=MESH)
    pl.semaphore_signal(barrier, inc=1, device_id={"row": 1 - r}, device_id_type=MESH)

    @pl.when(up)
    def _():
        pl.semaphore_signal(barrier, inc=1, device_id={"col": c + 1}, device_id_type=MESH)

    @pl.when(down)
    def _():
        pl.semaphore_signal(barrier, inc=1, device_id={"col": c - 1}, device_id_type=MESH)

    def span(tok, col):
        return pl.ds(pl.multiple_of((tok * m + col) * rows, rows), rows)

    def at_slot(tok, side):
        return held.at[:, pl.ds(pl.multiple_of((tok * 2 + side) * chunk, chunk), chunk)]

    own = every.at[span(k, c), :]
    enter = pltpu.make_async_copy(acts, stage, local_sem.at[0])
    enter_g = pltpu.make_async_copy(grads.at[k], stage_g, local_sem.at[1])
    leave = pltpu.make_async_copy(stage, own, local_sem.at[2])
    leave_g = pltpu.make_async_copy(stage_g, at_slot(k, r), local_sem.at[3])

    @pl.when(up & down)
    def _():
        pl.semaphore_wait(barrier, n + 2)

    @pl.when(jnp.logical_not(up & down))
    def _():
        pl.semaphore_wait(barrier, n + 1)

    def z_copy(item, tok, col, way, fresh=False):
        begin = 0 if isinstance(item, int) and item == 0 else 2 * quarter
        cols = pl.ds(begin, 2 * quarter)
        where = every.at[span(tok, col), cols]
        return pltpu.make_async_remote_copy(
            acts.at[:, cols] if fresh else where, where,
            zsend.at[way, item, col], zrecv.at[item, col],
            device_id={"col": c + 1 - 2 * way}, device_id_type=MESH)

    def z_start(item, tok, fresh=False):
        @pl.when(up)
        def _():
            z_copy(item, tok, c, 0, fresh).start()

        @pl.when(down)
        def _():
            z_copy(item, tok, c, 1, fresh).start()

    def z_round(s, item, tok):
        below, above = c - 1 - s, c + 1 + s

        @pl.when(below >= 0)
        def _():
            z_copy(item, tok, below, 0).wait_recv()

            @pl.when(up)
            def _():
                z_copy(item, tok, below, 0).start()

        @pl.when(above < m)
        def _():
            z_copy(item, tok, above, 1).wait_recv()

            @pl.when(down)
            def _():
                z_copy(item, tok, above, 1).start()

    def ring_copy(line, col, offset, half, way, fresh=False):
        begin = 2 * quarter if isinstance(line, int) and line == m else 0
        cols = pl.ds(begin + half * quarter, quarter)
        tok = member(offset)
        where = every.at[span(tok, col), cols]
        return pltpu.make_async_remote_copy(
            acts.at[:, cols] if fresh else where, where,
            rsend.at[way, line, tok, half], rrecv.at[line, tok, half],
            device_id={"tok": member(1 - 2 * way)}, device_id_type=MESH)

    def ring_start(line, col, fresh=False):
        for half in range(2):
            for way in range(2):
                which = half if way == 0 else 1 - half
                if reach[which][way] >= 1:
                    ring_copy(line, col, 0, which, way, fresh).start()

    def ring_step(line, col, t):
        for half in range(2):
            for way in range(2):
                which = half if way == 0 else 1 - half
                if reach[which][way] >= t:
                    offset = -t if way == 0 else t
                    ring_copy(line, col, offset, which, way).wait_recv()
                    if reach[which][way] > t:
                        ring_copy(line, col, offset, which, way).start()

    def ring_sent(line, col):
        for half in range(2):
            for way in range(2):
                for t in range(reach[half][way]):
                    ring_copy(line, col, -t if way == 0 else t, half, way).wait_send()

    def at_distance(d, do):
        @pl.when(c - d >= 0)
        def _():
            do(c - d, c - d)

        @pl.when((c + d < m) & (d > 0))
        def _():
            do(c + d, c + d)

    def g_send(j):
        to = (k + j) % n
        return pltpu.make_async_remote_copy(
            grads.at[to], at_slot(k, r), gsend.at[j], grecv.at[k, r],
            device_id={"tok": to}, device_id_type=MESH)

    def g_recv(tok):
        where = at_slot(tok, r)
        return pltpu.make_async_remote_copy(
            where, where, gsend.at[0], grecv.at[tok, r],
            device_id={"row": 1 - r}, device_id_type=MESH)

    def partner(tok, side, fresh=False):
        where = at_slot(tok, side)
        return pltpu.make_async_remote_copy(
            grads.at[tok] if fresh else where, where, psend.at[tok], grecv.at[tok, side],
            device_id={"row": 1 - r}, device_id_type=MESH)

    ring_start(m, c, True)
    z_start(0, k, True)
    z_start(1, k, True)
    ring_start(c, c, True)
    partner(k, r, True).start()
    enter.start()
    enter_g.start()
    enter.wait()
    leave.start()
    enter_g.wait()
    leave_g.start()
    for t in range(1, hops + 1):
        ring_step(m, c, t)
        if t == 1:
            for j in sorted(range(1, n), key=lambda j: (min(j, n - j), j)):
                g_send(j).start()
        z_start(1 + (n - t), member(-t))
        if 2 * t != n:
            z_start(1 + t, member(t))

    def item_order():
        order = [0]
        for t in range(1, hops + 1):
            order.append(n - t)
            if 2 * t != n:
                order.append(t)
        return order

    def whole_round(s):
        z_round(s, 0, k)
        at_distance(s + 1, ring_start)
        for j in item_order():
            z_round(s, 1 + j, member(j))

    @pl.loop(0, m - 2)
    def _(s):
        whole_round(s)

    for j in sorted(range(1, n), key=lambda j: (min(j, n - j), j)):
        tok = (k + n - j) % n
        g_recv(tok).wait_recv()
        partner(tok, r).start()

    @pl.loop(0, m - 1)
    def _(d):
        at_distance(d, functools.partial(ring_step, t=1))

    @pl.loop(0, n)
    def _(j):
        partner((k + j) % n, 1 - r).wait_recv()

    z_round(m - 2, 0, k)
    at_distance(m - 1, ring_start)
    at_distance(m - 1, functools.partial(ring_step, t=1))
    for j in item_order():
        z_round(m - 2, 1 + j, member(j))
    for t in range(2, hops + 1):
        @pl.loop(0, m)
        def _(d):
            at_distance(d, functools.partial(ring_step, t=t))

    for j in range(1, n):
        g_send(j).wait_send()

    @pl.loop(0, n)
    def _(j):
        partner(j, r).wait_send()

    ring_sent(m, c)

    @pl.loop(0, m)
    def _(d):
        at_distance(d, ring_sent)

    def z_sent(item, tok):
        @pl.loop(0, m)
        def _(col):
            @pl.when((col <= c) & up)
            def _():
                z_copy(item, tok, col, 0).wait_send()

            @pl.when((col >= c) & down)
            def _():
                z_copy(item, tok, col, 1).wait_send()

    z_sent(0, k)
    for j in range(n):
        z_sent(1 + j, member(j))
    leave.wait()
    leave_g.wait()


def body(n, m, activations, grads_t):
    _, units, chunk = grads_t.shape
    rows, wide = activations.shape
    tokens = rows * n * m
    dma = pltpu.SemaphoreType.DMA
    every, held = pl.pallas_call(
        functools.partial(kernel, n, m),
        out_shape=(
            jax.ShapeDtypeStruct((tokens, wide), jnp.bfloat16),
            jax.ShapeDtypeStruct((units, n * 2 * chunk), jnp.bfloat16),
        ),
        in_specs=[pl.BlockSpec(memory_space=pl.ANY)] * 2,
        out_specs=[pl.BlockSpec(memory_space=pl.ANY)] * 2,
        scratch_shapes=[
            pltpu.VMEM((rows, wide), jnp.bfloat16),
            pltpu.VMEM((units, chunk), jnp.bfloat16),
            dma((4,)),
            dma((2, n + 1, m)),
            dma((n + 1, m)),
            dma((2, m + 1, n, 2)),
            dma((m + 1, n, 2)),
            dma((n,)),
            dma((n, 2)),
            dma((n,)),
        ],
        compiler_params=pltpu.CompilerParams(
            collective_id=0, has_side_effects=True, vmem_limit_bytes=60 * 2**20),
    )(activations, grads_t)
    return jnp.dot(held, every, preferred_element_type=jnp.float32)[None]


def solution(mesh):
    return jax.shard_map(
        functools.partial(body, mesh.shape["tok"], mesh.shape["col"]),
        mesh=mesh,
        in_specs=(P(("tok", "col"), "row"), P(None, "col", ("tok", "row"))),
        out_specs=P("tok", "col", "row"),
        check_vma=False,
    )
```

profile of v0, /device:TPU:0, one launch (start us, length us, event | category | flops | bytes accessed | tf_op | source)
XLA Modules:
  0.0 115.3 jit_solution(2143651731753043305)
XLA Ops:
  0.0 93.1 %shard_map.28 = (bf16[2048,2048]{1,0:T(8,128)(2,1)}, bf16[1848,2048]{1,0:T(8,128)(2,1)}) custom-call(bf16[128,2048]{1,0:T(8,128)(2,1)} %acts.1, bf16[4,1848,256]{2,1,0:T(8,128)(2,1)} %grads.1), custom_call_target="tpu_custom_call" | custom-call | tf_op jit(solution)/shard_map/pallas_call | solution.py:260
  93.1 22.2 %convolution_bitcast_fusion = f32[1,1848,2048]{2,1,0:T(8,128)} fusion(bf16[1848,2048]{1,0:T(8,128)(2,1)} %get-tuple-element.7, bf16[2048,2048]{1,0:T(8,128)(2,1)} %get-tuple-element.8), kind=kOutput, calls=%fused_computation | convolution fusion | flops 15502147584 | bytes 31096832 | tf_op jit(solution)/shard_map/dot_general | solution.py:283
where the time goes:
time: 115 us
  Pallas kernels  93.1 us (81%)
  matrix products  22.2 us (19%)
    pallas_call x1, Pallas kernels, body(): pl.pallas_call(functools.partial(kernel, n, m), out_shape=(jax.ShapeDtype...  93.1 us
    dot_general x1, matrix products, body(): return jnp.dot(held, every, preferred_element_type=jnp.float32)[None]  22.2 us

commit v1 on v0

--- a/solution.py
+++ b/solution.py
@@ -8,12 +8,311 @@
 from jax.sharding import PartitionSpec as P
 
 MESH = pl.DeviceIdType.MESH
+TILE = 256
+SLOTS = 3
 
 
 def ring_map(place, n):
     if n % 4:
         return place
     return place + ((place % 4) // 2) * (1 - 2 * (place % 2))
+
+
+def plane_at(q, c, m):
+    near = jnp.minimum(c, m - 1 - c)
+    away = jnp.where(2 * c < m, 1, -1)
+    both = away * ((q + 1) // 2) if q % 2 else -away * (q // 2)
+    return c + jnp.where(q <= 2 * near, both, away * (q - near))
+
+
+def plane_dot(n, m, rows, every, held, plane, cols):
+    chunk = held.shape[2]
+    side = plane * rows // chunk
+    lanes = pl.ds(pl.multiple_of(plane * rows % chunk, rows), rows)
+    left = [held[2 * tok + side, :, lanes] for tok in range(n)]
+    right = [every[pl.ds(pl.multiple_of((tok * m + plane) * rows, rows), rows), cols] for tok in range(n)]
+    return jnp.dot(
+        jnp.concatenate(left, axis=1), jnp.concatenate(right, axis=0),
+        preferred_element_type=jnp.float32)
+
+
+def finish(n, m, every, held, acc, out, tile, sem):
+    rows = every.shape[0] // (n * m)
+    slots, _, width = tile.shape
+    steps = acc.shape[1] // width
+    plane = plane_at(m - 1, lax.axis_index("col"), m)
+
+    def leave(i):
+        cols = pl.ds(pl.multiple_of(i * width, width), width)
+        return pltpu.make_async_copy(tile.at[i % slots], out.at[0, :, cols], sem.at[i % slots])
+
+    @pl.loop(0, steps)
+    def _(i):
+        @pl.when(i >= slots)
+        def _():
+            leave(i - slots).wait()
+
+        cols = pl.ds(pl.multiple_of(i * width, width), width)
+        tile[i % slots] = acc[:, cols] + plane_dot(n, m, rows, every, held, plane, cols)
+        leave(i).start()
+
+    @pl.loop(max(0, steps - slots), steps)
+    def _(i):
+        leave(i).wait()
+
+
+def fused(n, m, acts, grads, every, held, acc,
+          local_sem, zsend, zrecv, rsend, rrecv, gsend, grecv, psend):
+    k, r, c = lax.axis_index("tok"), lax.axis_index("row"), lax.axis_index("col")
+    place = ring_map(k, n)
+    rows, wide = acts.shape
+    quarter = wide // 4
+    chunk = grads.shape[2]
+    up, down = c + 1 < m, c > 0
+    reach = ((n // 2, n - 1 - n // 2), (n - 1 - n // 2, n // 2))
+    hops = n // 2
+
+    def member(offset):
+        return ring_map((place + offset + 2 * n) % n, n)
+
+    barrier = pltpu.get_barrier_semaphore()
+    for j in range(1, n):
+        pl.semaphore_signal(barrier, inc=1, device_id={"tok": (k + j) % n}, device_id_type=MESH)
+    pl.semaphore_signal(barrier, inc=1, device_id={"row": 1 - r}, device_id_type=MESH)
+
+    @pl.when(up)
+    def _():
+        pl.semaphore_signal(barrier, inc=1, device_id={"col": c + 1}, device_id_type=MESH)
+
+    @pl.when(down)
+    def _():
+        pl.semaphore_signal(barrier, inc=1, device_id={"col": c - 1}, device_id_type=MESH)
+
+    def span(tok, col):
+        return pl.ds(pl.multiple_of((tok * m + col) * rows, rows), rows)
+
+    def at_slot(tok, side):
+        return held.at[tok * 2 + side]
+
+    own = every.at[span(k, c), :]
+    enter = pltpu.make_async_copy(acts, own, local_sem.at[0])
+    enter_g = pltpu.make_async_copy(grads.at[k], at_slot(k, r), local_sem.at[1])
+
+    @pl.when(up & down)
+    def _():
+        pl.semaphore_wait(barrier, n + 2)
+
+    @pl.when(jnp.logical_not(up & down))
+    def _():
+        pl.semaphore_wait(barrier, n + 1)
+
+    def z_copy(item, tok, col, way, fresh=False):
+        begin = 0 if isinstance(item, int) and item == 0 else 2 * quarter
+        cols = pl.ds(begin, 2 * quarter)
+        where = every.at[span(tok, col), cols]
+        return pltpu.make_async_remote_copy(
+            acts.at[:, cols] if fresh else where, where,
+            zsend.at[way, item, col], zrecv.at[item, col],
+            device_id={"col": c + 1 - 2 * way}, device_id_type=MESH)
+
+    def z_start(item, tok, fresh=False):
+        @pl.when(up)
+        def _():
+            z_copy(item, tok, c, 0, fresh).start()
+
+        @pl.when(down)
+        def _():
+            z_copy(item, tok, c, 1, fresh).start()
+
+    def z_round(s, item, tok):
+        below, above = c - 1 - s, c + 1 + s
+
+        @pl.when(below >= 0)
+        def _():
+            z_copy(item, tok, below, 0).wait_recv()
+
+            @pl.when(up)
+            def _():
+                z_copy(item, tok, below, 0).start()
+
+        @pl.when(above < m)
+        def _():
+            z_copy(item, tok, above, 1).wait_recv()
+
+            @pl.when(down)
+            def _():
+                z_copy(item, tok, above, 1).start()
+
+    def ring_copy(line, col, offset, half, way, fresh=False):
+        begin = 2 * quarter if isinstance(line, int) and line == m else 0
+        cols = pl.ds(begin + half * quarter, quarter)
+        tok = member(offset)
+        where = every.at[span(tok, col), cols]
+        return pltpu.make_async_remote_copy(
+            acts.at[:, cols] if fresh else where, where,
+            rsend.at[way, line, tok, half], rrecv.at[line, tok, half],
+            device_id={"tok": member(1 - 2 * way)}, device_id_type=MESH)
+
+    def ring_start(line, col, fresh=False):
+        for half in range(2):
+            for way in range(2):
+                which = half if way == 0 else 1 - half
+                if reach[which][way] >= 1:
+                    ring_copy(line, col, 0, which, way, fresh).start()
+
+    def ring_step(line, col, t):
+        for half in range(2):
+            for way in range(2):
+                which = half if way == 0 else 1 - half
+                if reach[which][way] >= t:
+                    offset = -t if way == 0 else t
+                    ring_copy(line, col, offset, which, way).wait_recv()
+                    if reach[which][way] > t:
+                        ring_copy(line, col, offset, which, way).start()
+
+    def ring_sent(line, col):
+        for half in range(2):
+            for way in range(2):
+                for t in range(reach[half][way]):
+                    ring_copy(line, col, -t if way == 0 else t, half, way).wait_send()
+
+    def at_distance(d, do):
+        @pl.when(c - d >= 0)
+        def _():
+            do(c - d, c - d)
+
+        @pl.when((c + d < m) & (d > 0))
+        def _():
+            do(c + d, c + d)
+
+    def g_send(j):
+        to = (k + j) % n
+        return pltpu.make_async_remote_copy(
+            grads.at[to], at_slot(k, r), gsend.at[j], grecv.at[k, r],
+            device_id={"tok": to}, device_id_type=MESH)
+
+    def g_recv(tok):
+        where = at_slot(tok, r)
+        return pltpu.make_async_remote_copy(
+            where, where, gsend.at[0], grecv.at[tok, r],
+            device_id={"row": 1 - r}, device_id_type=MESH)
+
+    def partner(tok, side, fresh=False):
+        where = at_slot(tok, side)
+        return pltpu.make_async_remote_copy(
+            grads.at[tok] if fresh else where, where, psend.at[tok], grecv.at[tok, side],
+            device_id={"row": 1 - r}, device_id_type=MESH)
+
+    ring_start(m, c, True)
+    z_start(0, k, True)
+    z_start(1, k, True)
+    ring_start(c, c, True)
+    partner(k, r, True).start()
+    enter.start()
+    enter_g.start()
+    enter.wait()
+    enter_g.wait()
+    for t in range(1, hops + 1):
+        ring_step(m, c, t)
+        if t == 1:
+            for j in sorted(range(1, n), key=lambda j: (min(j, n - j), j)):
+                g_send(j).start()
+        z_start(1 + (n - t), member(-t))
+        if 2 * t != n:
+            z_start(1 + t, member(t))
+
+    def item_order():
+        order = [0]
+        for t in range(1, hops + 1):
+            order.append(n - t)
+            if 2 * t != n:
+                order.append(t)
+        return order
+
+    def whole_round(s):
+        z_round(s, 0, k)
+        at_distance(s + 1, ring_start)
+        for j in item_order():
+            z_round(s, 1 + j, member(j))
+
+    @pl.loop(0, m - 2)
+    def _(s):
+        whole_round(s)
+
+    for j in sorted(range(1, n), key=lambda j: (min(j, n - j), j)):
+        tok = (k + n - j) % n
+        g_recv(tok).wait_recv()
+        partner(tok, r).start()
+
+    @pl.loop(0, m - 1)
+    def _(d):
+        at_distance(d, functools.partial(ring_step, t=1))
+
+    @pl.loop(0, n)
+    def _(j):
+        partner((k + j) % n, 1 - r).wait_recv()
+
+    tiles = wide // TILE
+
+    def multiply(q, half):
+        plane = plane_at(q, c, m)
+
+        @pl.loop(half * tiles // 2, (half + 1) * tiles // 2)
+        def _(i):
+            cols = pl.ds(pl.multiple_of(i * TILE, TILE), TILE)
+            part = plane_dot(n, m, rows, every, held, plane, cols)
+            acc[:, cols] = part if q == 0 else acc[:, cols] + part
+
+    def last_hops(d):
+        for t in range(2, hops + 1):
+            at_distance(d, functools.partial(ring_step, t=t))
+
+    multiply(0, 1)
+    z_round(m - 2, 0, k)
+    at_distance(m - 1, ring_start)
+    if m > 2:
+        multiply(1, 1)
+    at_distance(m - 1, functools.partial(ring_step, t=1))
+    for place_in_order, j in enumerate(item_order()):
+        z_round(m - 2, 1 + j, member(j))
+        if place_in_order == 0:
+            for q in range(2, m - 1):
+                multiply(q, 1)
+        if place_in_order < m - 1:
+            last_hops(place_in_order)
+            multiply(place_in_order, 0)
+    for q in range(n, m - 1):
+        last_hops(q)
+        multiply(q, 0)
+    last_hops(m - 1)
+
+    for j in range(1, n):
+        g_send(j).wait_send()
+
+    @pl.loop(0, n)
+    def _(j):
+        partner(j, r).wait_send()
+
+    ring_sent(m, c)
+
+    @pl.loop(0, m)
+    def _(d):
+        at_distance(d, ring_sent)
+
+    def z_sent(item, tok):
+        @pl.loop(0, m)
+        def _(col):
+            @pl.when((col <= c) & up)
+            def _():
+                z_copy(item, tok, col, 0).wait_send()
+
+            @pl.when((col >= c) & down)
+            def _():
+                z_copy(item, tok, col, 1).wait_send()
+
+    z_sent(0, k)
+    for j in range(n):
+        z_sent(1 + j, member(j))
 
 
 def kernel(n, m, acts, grads, every, held, stage, stage_g,
@@ -252,7 +551,7 @@
     leave_g.wait()
 
 
-def body(n, m, activations, grads_t):
+def plain_body(n, m, activations, grads_t):
     _, units, chunk = grads_t.shape
     rows, wide = activations.shape
     tokens = rows * n * m
@@ -283,6 +582,59 @@
     return jnp.dot(held, every, preferred_element_type=jnp.float32)[None]
 
 
+def semaphores(n, m):
+    dma = pltpu.SemaphoreType.DMA
+    return [
+        dma((4,)),
+        dma((2, n + 1, m)),
+        dma((n + 1, m)),
+        dma((2, m + 1, n, 2)),
+        dma((m + 1, n, 2)),
+        dma((n,)),
+        dma((n, 2)),
+        dma((n,)),
+    ]
+
+
+def fused_body(n, m, activations, grads_t):
+    _, units, chunk = grads_t.shape
+    rows, wide = activations.shape
+    every, held, acc = pl.pallas_call(
+        functools.partial(fused, n, m),
+        out_shape=(
+            pltpu.VMEM((rows * n * m, wide), jnp.bfloat16),
+            pltpu.VMEM((n * 2, units, chunk), jnp.bfloat16),
+            pltpu.VMEM((units, wide), jnp.float32),
+        ),
+        in_specs=[pl.BlockSpec(memory_space=pl.ANY)] * 2,
+        out_specs=[pl.BlockSpec(memory_space=pltpu.VMEM)] * 3,
+        scratch_shapes=semaphores(n, m),
+        compiler_params=pltpu.CompilerParams(
+            collective_id=0, has_side_effects=True, vmem_limit_bytes=26 * 2**20),
+    )(activations, grads_t)
+    return pl.pallas_call(
+        functools.partial(finish, n, m),
+        out_shape=jax.ShapeDtypeStruct((1, units, wide), jnp.float32),
+        in_specs=[pl.BlockSpec(memory_space=pltpu.VMEM)] * 3,
+        out_specs=pl.BlockSpec(memory_space=pl.ANY),
+        scratch_shapes=[
+            pltpu.VMEM((SLOTS, units, TILE), jnp.float32),
+            pltpu.SemaphoreType.DMA((SLOTS,)),
+        ],
+        compiler_params=pltpu.CompilerParams(vmem_limit_bytes=20 * 2**20),
+    )(every, held, acc)
+
+
+def body(n, m, activations, grads_t):
+    _, units, chunk = grads_t.shape
+    rows, wide = activations.shape
+    resident = 2 * n * units * chunk * 2 + rows * n * m * wide * 2 + units * wide * 4
+    fits = rows % 128 == 0 and chunk % rows == 0 and wide % (2 * TILE) == 0
+    if fits and m > 1 and resident <= 32 * 2**20:
+        return fused_body(n, m, activations, grads_t)
+    return plain_body(n, m, activations, grads_t)
+
+
 def solution(mesh):
     return jax.shard_map(
         functools.partial(body, mesh.shape["tok"], mesh.shape["col"]),

time: 115 us -> 110 us (0.957)
  the two profiles are of different devices: /device:TPU:0 before, /device:TPU:1 now
where the time goes in v1:
time: 110 us
  Pallas kernels  110 us (100%)
    pallas_call x1, Pallas kernels, fused_body(): pl.pallas_call(functools.partial(fused, n, m), out_shape=(pltpu.VMEM((row...  103 us
    pallas_call x1, Pallas kernels, fused_body(): pl.pallas_call(functools.partial(finish, n, m), out_shape=jax.ShapeDtypeS...  6.9 us

profile of v1, /device:TPU:1, one launch (start us, length us, event | category | flops | bytes accessed | tf_op | source)
XLA Modules:
  0.0 109.8 jit_solution(2351609291640087866)
XLA Ops:
  0.0 102.8 %shard_map.28 = (bf16[2048,2048]{1,0:T(8,128)(2,1)S(1)}, bf16[8,1848,256]{2,1,0:T(8,128)(2,1)S(1)}, f32[1848,2048]{1,0:T(8,128)S(1)}) custom-call(bf16[128,2048]{1,0:T(8,128)(2,1)} %acts.1, bf16[4,1848,256]{2,1,0:T(8,128)(2,1)} %grads.1), custom_call_target="tpu_custom_call" | custom-call | tf_op jit(solution)/shard_map/pallas_call | solution.py:602
  102.9 6.9 %shard_map.29 = f32[1,1848,2048]{2,1,0:T(8,128)} custom-call(bf16[2048,2048]{1,0:T(8,128)(2,1)S(1)} %get-tuple-element.8.every, bf16[8,1848,256]{2,1,0:T(8,128)(2,1)S(1)} %get-tuple-element.9.held, f32[1848,2048]{1,0:T(8,128)S(1)} %get-tuple-element.10.acc), custom_call_target="tpu_custom_call" | custom-call | tf_op jit(solution)/shard_map/pallas_call | solution.py:615

commit v2 on v1

--- a/solution.py
+++ b/solution.py
@@ -66,6 +66,7 @@
     k, r, c = lax.axis_index("tok"), lax.axis_index("row"), lax.axis_index("col")
     place = ring_map(k, n)
     rows, wide = acts.shape
+    units = grads.shape[1]
     quarter = wide // 4
     chunk = grads.shape[2]
     up, down = c + 1 < m, c > 0
@@ -185,11 +186,20 @@
         def _():
             do(c + d, c + d)
 
-    def g_send(j):
+    pieces = max(p for p in range(1, 9) if units % (8 * p) == 0)
+    others = sorted(range(1, n), key=lambda j: (min(j, n - j), j))
+
+    def g_send(j, piece=None):
         to = (k + j) % n
-        return pltpu.make_async_remote_copy(
-            grads.at[to], at_slot(k, r), gsend.at[j], grecv.at[k, r],
+        part = (pl.ds(0, units) if piece is None
+                else pl.ds(piece * (units // pieces), units // pieces))
+        return pltpu.make_async_remote_copy(
+            grads.at[to, part], at_slot(k, r).at[part], gsend.at[j], grecv.at[k, r],
             device_id={"tok": to}, device_id_type=MESH)
+
+    def g_start(piece):
+        for j in others:
+            g_send(j, piece).start()
 
     def g_recv(tok):
         where = at_slot(tok, r)
@@ -202,11 +212,59 @@
         return pltpu.make_async_remote_copy(
             grads.at[tok] if fresh else where, where, psend.at[tok], grecv.at[tok, side],
             device_id={"row": 1 - r}, device_id_type=MESH)
+
+    tiles = wide // TILE
+
+    def multiply(q, half):
+        plane = plane_at(q, c, m)
+
+        @pl.loop(half * tiles // 2, (half + 1) * tiles // 2)
+        def _(i):
+            cols = pl.ds(pl.multiple_of(i * TILE, TILE), TILE)
+            part = plane_dot(n, m, rows, every, held, plane, cols)
+            acc[:, cols] = part if (q, half) in first else acc[:, cols] + part
+
+    first = ((0, 0), (0, 1))
+
+    def line_start(d):
+        at_distance(d, ring_start)
+
+    def line_step(d, t):
+        at_distance(d, functools.partial(ring_step, t=t))
+
+    def pass_grads():
+        for j in others:
+            tok = (k + n - j) % n
+            g_recv(tok).wait_recv()
+            partner(tok, r).start()
+
+    def all_grads():
+        for j in range(n):
+            partner((k + j) % n, 1 - r).wait_recv()
+
+    per_round = n + 1
+    plan = []
+    for p in range(2, pieces):
+        plan.append((p - 1, 1, functools.partial(g_start, p)))
+    passed = pieces + 1
+    plan.append((passed, 2, pass_grads))
+    plan.append((passed + 1, 2, all_grads))
+    for d in range(m):
+        begin = max(pieces - 1 + d, (d - 1) * per_round)
+        plan.append((begin, 1, functools.partial(line_start, d)))
+        plan.append((begin + 3, 0, functools.partial(line_step, d, 1)))
+        for t in range(2, hops + 1):
+            plan.append((begin + 1 + 2 * t, 0, functools.partial(line_step, d, t)))
+        if d < m - 1:
+            there = max(passed + 1 + d, d * per_round - 1)
+            plan.append((there, 3, functools.partial(multiply, d, 1)))
+            there = max(there, begin + 1 + 2 * hops)
+            plan.append((there, 4, functools.partial(multiply, d, 0)))
+    plan.sort(key=lambda entry: entry[:2])
 
     ring_start(m, c, True)
     z_start(0, k, True)
     z_start(1, k, True)
-    ring_start(c, c, True)
     partner(k, r, True).start()
     enter.start()
     enter_g.start()
@@ -214,77 +272,26 @@
     enter_g.wait()
     for t in range(1, hops + 1):
         ring_step(m, c, t)
-        if t == 1:
-            for j in sorted(range(1, n), key=lambda j: (min(j, n - j), j)):
-                g_send(j).start()
+        if t <= min(2, pieces):
+            g_start(t - 1)
         z_start(1 + (n - t), member(-t))
         if 2 * t != n:
             z_start(1 + t, member(t))
-
-    def item_order():
-        order = [0]
-        for t in range(1, hops + 1):
-            order.append(n - t)
-            if 2 * t != n:
-                order.append(t)
-        return order
-
-    def whole_round(s):
-        z_round(s, 0, k)
-        at_distance(s + 1, ring_start)
-        for j in item_order():
-            z_round(s, 1 + j, member(j))
-
-    @pl.loop(0, m - 2)
-    def _(s):
-        whole_round(s)
-
-    for j in sorted(range(1, n), key=lambda j: (min(j, n - j), j)):
-        tok = (k + n - j) % n
-        g_recv(tok).wait_recv()
-        partner(tok, r).start()
-
-    @pl.loop(0, m - 1)
-    def _(d):
-        at_distance(d, functools.partial(ring_step, t=1))
-
-    @pl.loop(0, n)
-    def _(j):
-        partner((k + j) % n, 1 - r).wait_recv()
-
-    tiles = wide // TILE
-
-    def multiply(q, half):
-        plane = plane_at(q, c, m)
-
-        @pl.loop(half * tiles // 2, (half + 1) * tiles // 2)
-        def _(i):
-            cols = pl.ds(pl.multiple_of(i * TILE, TILE), TILE)
-            part = plane_dot(n, m, rows, every, held, plane, cols)
-            acc[:, cols] = part if q == 0 else acc[:, cols] + part
-
-    def last_hops(d):
-        for t in range(2, hops + 1):
-            at_distance(d, functools.partial(ring_step, t=t))
-
-    multiply(0, 1)
-    z_round(m - 2, 0, k)
-    at_distance(m - 1, ring_start)
-    if m > 2:
-        multiply(1, 1)
-    at_distance(m - 1, functools.partial(ring_step, t=1))
-    for place_in_order, j in enumerate(item_order()):
-        z_round(m - 2, 1 + j, member(j))
-        if place_in_order == 0:
-            for q in range(2, m - 1):
-                multiply(q, 1)
-        if place_in_order < m - 1:
-            last_hops(place_in_order)
-            multiply(place_in_order, 0)
-    for q in range(n, m - 1):
-        last_hops(q)
-        multiply(q, 0)
-    last_hops(m - 1)
+    for p in range(hops, min(2, pieces)):
+        g_start(p)
+
+    items = [(0, k)]
+    for t in range(1, hops + 1):
+        items.append((1 + n - t, member(-t)))
+        if 2 * t != n:
+            items.append((1 + t, member(t)))
+    items.insert(1, (1, k))
+    for slot in range((m - 1) * per_round):
+        z_round(slot // per_round, *items[slot % per_round])
+        while plan and plan[0][0] <= slot:
+            plan.pop(0)[2]()
+    for _, _, act in plan:
+        act()
 
     for j in range(1, n):
         g_send(j).wait_send()

time: 110 us -> 99.8 us (0.907)
  the two profiles are of different devices: /device:TPU:1 before, /device:TPU:0 now
where the time goes in v2:
time: 99.8 us; the launch traced here: 99.5 us
  Pallas kernels  99.5 us (100%)
    pallas_call x1, Pallas kernels, fused_body(): pl.pallas_call(functools.partial(fused, n, m), out_shape=(pltpu.VMEM((row...  92.6 us
    pallas_call x1, Pallas kernels, fused_body(): pl.pallas_call(functools.partial(finish, n, m), out_shape=jax.ShapeDtypeS...  6.89 us

profile of v2, /device:TPU:0, one launch (start us, length us, event | category | flops | bytes accessed | tf_op | source)
XLA Modules:
  0.0 99.5 jit_solution(7354863009732960502)
XLA Ops:
  0.0 92.6 %shard_map.28 = (bf16[2048,2048]{1,0:T(8,128)(2,1)S(1)}, bf16[8,1848,256]{2,1,0:T(8,128)(2,1)S(1)}, f32[1848,2048]{1,0:T(8,128)S(1)}) custom-call(bf16[128,2048]{1,0:T(8,128)(2,1)} %acts.1, bf16[4,1848,256]{2,1,0:T(8,128)(2,1)} %grads.1), custom_call_target="tpu_custom_call" | custom-call | tf_op jit(solution)/shard_map/pallas_call | solution.py:609
  92.6 6.9 %shard_map.29 = f32[1,1848,2048]{2,1,0:T(8,128)} custom-call(bf16[2048,2048]{1,0:T(8,128)(2,1)S(1)} %get-tuple-element.8.every, bf16[8,1848,256]{2,1,0:T(8,128)(2,1)S(1)} %get-tuple-element.9.held, f32[1848,2048]{1,0:T(8,128)S(1)} %get-tuple-element.10.acc), custom_call_target="tpu_custom_call" | custom-call | tf_op jit(solution)/shard_map/pallas_call | solution.py:622
